TPU v7x, 32 devices: a whole 2x2x4 slice. The times are simulated.
32 devices in a mesh: row: 4 (over x, core), col: 8 (over z, y).
Axes of the slice: x: 2, y: 2, z: 4, core: 2. Of those that a mesh axis runs over, the one named last changes fastest.
Arguments:
- benefit: int32 [4096, 16384], P('row', 'col'), may hold values from 0 to 269488127, as said below
- prices: int32 [16384], P('col'), may hold values from 0 to 4095
- assignment: int32 [4096], P('row'), may hold values from -1 to 16383, as said below
- epsilon: int32 [1], replicated, may hold values from 1 to 1024
Outputs:
- new_prices: int32 [16384], P('col')
- new_assignment: int32 [4096], P('row')
Inputs may be any that keep to these rules, and one draw needn't show every extreme that they name: `assignment`: each entry is -1 or an object index, and no two persons hold the same object. `benefit`: several objects may share a person's best value.
All inputs are finite; a program needn't handle non-finite values.
Results may differ from a plain program's by a relative error of at most 0.000001.
Values may be sent and summed in bfloat16 or wider, within the bound.
A program may use at most 64 MiB of HBM per device.

v0:
```python
import jax
import jax.numpy as jnp
from jax import lax
from jax.sharding import PartitionSpec as P

ROUNDS = 4


LOWEST = -2147483647
LARGEST = 2147483647


def merged(part, axis, combine):
    gathered = jax.tree.map(lambda a: lax.all_gather(a, axis), part)

    def take(source):
        return jax.tree.map(lambda a: lax.dynamic_index_in_dim(a, source, 0, False), gathered)

    return lax.fori_loop(
        1, lax.axis_size(axis), lambda source, state: combine(state, take(source)), take(0)
    )


def pick_bids(first, second_one):
    bid_a, person_a = first
    bid_b, person_b = second_one
    take_a = (bid_a > bid_b) | (bid_a == bid_b) & (person_a < person_b)
    return (jnp.where(take_a, bid_a, bid_b), jnp.where(take_a, person_a, person_b))


def on_device(benefit, prices, assignment, epsilon):
    pers_rows = benefit.shape[0]
    obj_cols = benefit.shape[1]
    col_start = lax.axis_index("col") * obj_cols
    row_start = lax.axis_index("row") * pers_rows
    columns = jnp.arange(obj_cols, dtype=jnp.int32)
    persons = row_start + jnp.arange(pers_rows, dtype=jnp.int32)
    price = prices
    owner_of = assignment
    for step in range(ROUNDS):
        value = benefit - price[None, :]
        local_best = jnp.max(value, axis=1)
        local_arg = jnp.argmax(value, axis=1)
        local_second = jnp.max(
            jnp.where(columns[None, :] == local_arg[:, None], LOWEST, value), axis=1
        )
        local_target = col_start + local_arg
        best = lax.pmax(local_best, "col")
        target = lax.pmin(jnp.where(local_best == best, local_target, LARGEST), "col")
        share = jnp.where(local_target == target, local_second, local_best)
        second = lax.pmax(share, "col")
        free = owner_of < 0
        local_slot = target - col_start
        mine = free & (local_slot >= 0) & (local_slot < obj_cols)
        slot = jnp.where(mine, local_slot, obj_cols)
        safe_slot = jnp.clip(slot, 0, obj_cols - 1)
        target_price = jnp.where(mine, price[safe_slot], 0)
        bid = target_price + best - second + epsilon[0]
        block_bid = jnp.zeros((obj_cols,), jnp.int32).at[slot].max(bid, mode="drop")
        chosen = mine & (bid == block_bid[safe_slot])
        block_winner = (
            jnp.full((obj_cols,), LARGEST, jnp.int32)
            .at[jnp.where(chosen, slot, obj_cols)]
            .min(persons, mode="drop")
        )
        top_bid, winner = merged((block_bid, block_winner), "row", pick_bids)
        taken = top_bid > 0
        winner_pos = winner - row_start
        valid = taken & (winner_pos >= 0) & (winner_pos < pers_rows)
        won_object = (
            jnp.full((pers_rows,), -1, jnp.int32)
            .at[jnp.where(valid, winner_pos, pers_rows)]
            .max(col_start + columns, mode="drop")
        )
        held_slot = owner_of - col_start
        held_here = (owner_of >= 0) & (held_slot >= 0) & (held_slot < obj_cols)
        lost_here = (held_here & taken[jnp.clip(held_slot, 0, obj_cols - 1)]).astype(jnp.int32)
        won_all, lost_all = lax.pmax((won_object, lost_here), "col")
        owner_of = jnp.where(won_all >= 0, won_all, jnp.where(lost_all > 0, -1, owner_of))
        price = jnp.where(taken, top_bid, price)
    return (price, owner_of)


def solution(mesh):
    return jax.shard_map(
        on_device,
        mesh=mesh,
        in_specs=(P("row", "col"), P("col"), P("row"), P()),
        out_specs=(P("col"), P("row")),
        check_vma=False,
    )
```

profile of v0, /device:TPU:0, one launch (start us, length us, event | category | flops | bytes accessed | tf_op | source)
XLA Modules:
  0.0 463.4 jit_solution(13357846995416906195)
XLA Ops:
  0.6 0.0 copy-start
  0.6 0.0 copy-start.1
  0.7 0.0 copy-start.2
  0.7 7.2 %iota_reduce_fusion.3 = (s32[1024]{0:T(1024)}, s32[1024]{0:T(1024)S(1)}) fusion(s32[1024,2048]{1,0:T(8,128)} %param.12, s32[2048]{0:T(1024)} %param.13), kind=kLoop, calls=%fused_computation.55 | loop fusion | flops 16770048 | bytes 8404992 | tf_op jit(solution)/shard_map/on_device/reduce | solution.py:43
  7.9 0.0 copy-done
  7.9 0.0 copy-done.1
  7.9 2.9 select_reduce_fusion.3
  10.8 13.1 %pmax.112 = s32[1024]{0:T(1024)S(1)} all-reduce(s32[1024]{0:T(1024)S(1)} %get-tuple-element.557), channel_id=1, replica_groups=mesh['row'=4,'col'=8] {'col'}, use_global_device_ids=true, to_apply=%region_1.0 | all-reduce | flops 1024 | bytes 8192 | tf_op jit(solution)/shard_map/pmax | solution.py:48
  23.9 7.8 %pmin.28 = s32[1024]{0:T(1024)S(1)} all-reduce(s32[1024]{0:T(1024)S(1)} %compare_select_fusion.31), channel_id=1, replica_groups=mesh['row'=4,'col'=8] {'col'}, use_global_device_ids=true, to_apply=%region_3.4 | all-reduce | flops 1024 | bytes 8192 | tf_op jit(solution)/shard_map/pmin | solution.py:49
  31.7 6.2 %gather_fusion = s32[1024]{0:T(1024)S(1)} fusion(s32[2048]{0:T(1024)S(1)} %copy-done, s32[1024]{0:T(1024)S(1)} %get-tuple-element.629), kind=kCustom, calls=%fused_computation | custom fusion | bytes 12288 | tf_op jit(solution)/shard_map/gather | solution.py:57
  37.8 12.1 %pmax.113 = s32[1024]{0:T(1024)S(1)} all-reduce(s32[1024]{0:T(1024)S(1)} %get-tuple-element.648), channel_id=1, replica_groups=mesh['row'=4,'col'=8] {'col'}, use_global_device_ids=true, to_apply=%region_5.6 | all-reduce | flops 1024 | bytes 8192 | tf_op jit(solution)/shard_map/pmax | solution.py:51
  50.6 6.0 %scatter_custom_fusion = s32[2048]{0:T(1024)S(1)} fusion(s32[1024]{0:T(1024)S(1)} %get-tuple-element.656, s32[1024]{0:T(1024)S(1)} %get-tuple-element.655, s32[]{:T(128)} %constant.198.clone.1), kind=kCustom, calls=%fused_computation.116 | custom fusion | flops 1024 | bytes 8196 | tf_op jit(solution)/shard_map/scatter-max | solution.py:59
  56.7 6.2 %gather_fusion.1 = s32[1024]{0:T(1024)S(1)} fusion(s32[2048]{0:T(1024)S(1)} %scatter_custom_fusion, s32[1024]{0:T(1024)S(1)} %get-tuple-element.629), kind=kCustom, calls=%fused_computation.1 | custom fusion | bytes 12288 | tf_op jit(solution)/shard_map/gather | solution.py:60
  62.9 6.0 %scatter_custom_fusion.1 = s32[2048]{0:T(1024)S(1)} fusion(s32[1024]{0:T(1024)S(1)} %compare_select_fusion.21, s32[1024]{0:T(1024)S(1)} %iota_add_fusion.1, s32[]{:T(128)} %constant.203.clone.1), kind=kCustom, calls=%fused_computation.103 | custom fusion | flops 1024 | bytes 8196 | tf_op jit(solution)/shard_map/scatter-min | solution.py:64
  68.9 5.2 %all-gather.1 = s32[8192]{0:T(1024)S(1)} all-gather(s32[2048]{0:T(1024)S(1)} %scatter_custom_fusion.1), channel_id=3, replica_groups=mesh['row'=4,'col'=8] {'row'}, dimensions={0}, use_global_device_ids=true | all-gather | bytes 40960 | tf_op jit(solution)/shard_map/all_gather | solution.py:14
  74.1 5.4 %all-gather = s32[8192]{0:T(1024)S(1)} all-gather(s32[2048]{0:T(1024)S(1)} %scatter_custom_fusion), channel_id=2, replica_groups=mesh['row'=4,'col'=8] {'row'}, dimensions={0}, use_global_device_ids=true | all-gather | bytes 40960 | tf_op jit(solution)/shard_map/all_gather | solution.py:14
  79.5 0.2 while.68
  79.7 7.1 %iota_reduce_fusion.2 = (s32[1024]{0:T(1024)}, s32[1024]{0:T(1024)S(1)}) fusion(s32[1024,2048]{1,0:T(8,128)} %param.12, s32[2048]{0:T(1024)S(1)} %get-tuple-element.627), kind=kLoop, calls=%fused_computation.52 | loop fusion | flops 16770048 | bytes 8404992 | tf_op jit(solution)/shard_map/on_device/reduce | solution.py:43
  86.8 4.9 %select_reduce_fusion.2 = (s32[1024]{0:T(1024)S(1)}, s32[1024]{0:T(1024)S(1)}) fusion(s32[1024,2048]{1,0:T(8,128)} %param.12, s32[1024]{0:T(1024)S(1)} %get-tuple-element.541, s32[2048]{0:T(1024)S(1)} %get-tuple-element.627), kind=kLoop, calls=%fused_computation.50 | loop fusion | flops 10483712 | bytes 8409088 | tf_op jit(solution)/shard_map/reduce_max | solution.py:44
  91.6 8.0 %pmax.116 = s32[1024]{0:T(1024)S(1)} all-reduce(s32[1024]{0:T(1024)S(1)} %get-tuple-element.555), channel_id=1, replica_groups=mesh['row'=4,'col'=8] {'col'}, use_global_device_ids=true, to_apply=%region_14.15 | all-reduce | flops 1024 | bytes 8192 | tf_op jit(solution)/shard_map/pmax | solution.py:48
  99.7 11.8 %pmin.29 = s32[1024]{0:T(1024)S(1)} all-reduce(s32[1024]{0:T(1024)S(1)} %compare_select_fusion.29), channel_id=1, replica_groups=mesh['row'=4,'col'=8] {'col'}, use_global_device_ids=true, to_apply=%region_16.17 | all-reduce | flops 1024 | bytes 8192 | tf_op jit(solution)/shard_map/pmin | solution.py:49
  111.5 6.8 %gather_fusion.2 = pred[1024]{0:T(1024)(128)(4,1)S(1)} fusion(pred[2048]{0:T(1024)(128)(4,1)S(1)} %get-tuple-element.628, s32[1024]{0:T(1024)S(1)} %get-tuple-element.647), kind=kCustom, calls=%fused_computation.2 | custom fusion | bytes 6144 | tf_op jit(solution)/shard_map/gather | solution.py:77
  118.4 11.5 %scatter_custom_fusion.2 = s32[1024]{0:T(1024)S(1)} fusion(s32[2048]{0:T(1024)S(1)} %compare_select_fusion.3, s32[2048]{0:T(1024)S(1)} %iota_add_fusion, s32[]{:T(128)} %constant.199.clone.1), kind=kCustom, calls=%fused_computation.144 | custom fusion | flops 2048 | bytes 4100 | tf_op jit(solution)/shard_map/scatter-max | solution.py:73
  129.9 34.4 %all-reduce.3 = (s32[1024]{0:T(1024)S(1)}, s32[1024]{0:T(1024)S(1)}, s32[1024]{0:T(1024)S(1)}) all-reduce(s32[1024]{0:T(1024)S(1)} %scatter_custom_fusion.2, s32[1024]{0:T(1024)S(1)} %and_convert_fusion.3, s32[1024]{0:T(1024)S(1)} %compare_select_fusion.28), channel_id=1, replica_groups=mesh['row'=4,'col'=8] {'col'}, use_global_device_ids=true, to_apply=%region_11.12 | all-reduce | flops 3072 | bytes 24576 | tf_op jit(solution)/shard_map/pmax | solution.py:78
  164.3 6.2 %gather_fusion.3 = s32[1024]{0:T(1024)S(1)} fusion(s32[2048]{0:T(1024)S(1)} %get-tuple-element.627, s32[1024]{0:T(1024)S(1)} %get-tuple-element.625), kind=kCustom, calls=%fused_computation.3 | custom fusion | bytes 12288 | tf_op jit(solution)/shard_map/gather | solution.py:57
  170.5 6.0 %scatter_custom_fusion.3 = s32[2048]{0:T(1024)S(1)} fusion(s32[1024]{0:T(1024)S(1)} %get-tuple-element.654, s32[1024]{0:T(1024)S(1)} %get-tuple-element.653, s32[]{:T(128)} %constant.198.clone.1), kind=kCustom, calls=%fused_computation.111 | custom fusion | flops 1024 | bytes 8196 | tf_op jit(solution)/shard_map/scatter-max | solution.py:59
  176.5 6.2 %gather_fusion.4 = s32[1024]{0:T(1024)S(1)} fusion(s32[2048]{0:T(1024)S(1)} %scatter_custom_fusion.3, s32[1024]{0:T(1024)S(1)} %get-tuple-element.625), kind=kCustom, calls=%fused_computation.4 | custom fusion | bytes 12288 | tf_op jit(solution)/shard_map/gather | solution.py:60
  182.7 6.0 %scatter_custom_fusion.4 = s32[2048]{0:T(1024)S(1)} fusion(s32[1024]{0:T(1024)S(1)} %compare_select_fusion.16, s32[1024]{0:T(1024)S(1)} %iota_add_fusion.1, s32[]{:T(128)} %constant.203.clone.1), kind=kCustom, calls=%fused_computation.101 | custom fusion | flops 1024 | bytes 8196 | tf_op jit(solution)/shard_map/scatter-min | solution.py:64
  188.7 5.2 %all-gather.3 = s32[8192]{0:T(1024)S(1)} all-gather(s32[2048]{0:T(1024)S(1)} %scatter_custom_fusion.4), channel_id=5, replica_groups=mesh['row'=4,'col'=8] {'row'}, dimensions={0}, use_global_device_ids=true | all-gather | bytes 40960 | tf_op jit(solution)/shard_map/all_gather | solution.py:14
  194.0 5.4 %all-gather.2 = s32[8192]{0:T(1024)S(1)} all-gather(s32[2048]{0:T(1024)S(1)} %scatter_custom_fusion.3), channel_id=4, replica_groups=mesh['row'=4,'col'=8] {'row'}, dimensions={0}, use_global_device_ids=true | all-gather | bytes 40960 | tf_op jit(solution)/shard_map/all_gather | solution.py:14
  199.4 0.2 while.69
  199.6 7.1 %iota_reduce_fusion.1 = (s32[1024]{0:T(1024)}, s32[1024]{0:T(1024)S(1)}) fusion(s32[1024,2048]{1,0:T(8,128)} %param.12, s32[2048]{0:T(1024)S(1)} %get-tuple-element.621), kind=kLoop, calls=%fused_computation.49 | loop fusion | flops 16770048 | bytes 8404992 | tf_op jit(solution)/shard_map/on_device/reduce | solution.py:43
  206.7 4.9 %select_reduce_fusion.1 = (s32[1024]{0:T(1024)S(1)}, s32[1024]{0:T(1024)S(1)}) fusion(s32[1024,2048]{1,0:T(8,128)} %param.12, s32[1024]{0:T(1024)S(1)} %get-tuple-element.544, s32[2048]{0:T(1024)S(1)} %get-tuple-element.621), kind=kLoop, calls=%fused_computation.47 | loop fusion | flops 10483712 | bytes 8409088 | tf_op jit(solution)/shard_map/reduce_max | solution.py:44
  211.6 6.8 %pmax.120 = s32[1024]{0:T(1024)S(1)} all-reduce(s32[1024]{0:T(1024)S(1)} %get-tuple-element.553), channel_id=1, replica_groups=mesh['row'=4,'col'=8] {'col'}, use_global_device_ids=true, to_apply=%region_27.28 | all-reduce | flops 1024 | bytes 8192 | tf_op jit(solution)/shard_map/pmax | solution.py:48
  218.4 13.1 %pmin.30 = s32[1024]{0:T(1024)S(1)} all-reduce(s32[1024]{0:T(1024)S(1)} %compare_select_fusion.27), channel_id=1, replica_groups=mesh['row'=4,'col'=8] {'col'}, use_global_device_ids=true, to_apply=%region_29.30 | all-reduce | flops 1024 | bytes 8192 | tf_op jit(solution)/shard_map/pmin | solution.py:49
  231.5 6.8 %gather_fusion.5 = pred[1024]{0:T(1024)(128)(4,1)S(1)} fusion(pred[2048]{0:T(1024)(128)(4,1)S(1)} %get-tuple-element.622, s32[1024]{0:T(1024)S(1)} %get-tuple-element.623), kind=kCustom, calls=%fused_computation.5 | custom fusion | bytes 6144 | tf_op jit(solution)/shard_map/gather | solution.py:77
  238.3 11.5 %scatter_custom_fusion.5 = s32[1024]{0:T(1024)S(1)} fusion(s32[2048]{0:T(1024)S(1)} %compare_select_fusion.2, s32[2048]{0:T(1024)S(1)} %iota_add_fusion, s32[]{:T(128)} %constant.199.clone.1), kind=kCustom, calls=%fused_computation.142 | custom fusion | flops 2048 | bytes 4100 | tf_op jit(solution)/shard_map/scatter-max | solution.py:73
  249.8 33.0 %all-reduce.2 = (s32[1024]{0:T(1024)S(1)}, s32[1024]{0:T(1024)S(1)}, s32[1024]{0:T(1024)S(1)}) all-reduce(s32[1024]{0:T(1024)S(1)} %scatter_custom_fusion.5, s32[1024]{0:T(1024)S(1)} %and_convert_fusion.2, s32[1024]{0:T(1024)S(1)} %compare_select_fusion.26), channel_id=1, replica_groups=mesh['row'=4,'col'=8] {'col'}, use_global_device_ids=true, to_apply=%region_24.25 | all-reduce | flops 3072 | bytes 24576 | tf_op jit(solution)/shard_map/pmax | solution.py:78
  282.8 6.2 %gather_fusion.6 = s32[1024]{0:T(1024)S(1)} fusion(s32[2048]{0:T(1024)S(1)} %get-tuple-element.621, s32[1024]{0:T(1024)S(1)} %get-tuple-element.619), kind=kCustom, calls=%fused_computation.6 | custom fusion | bytes 12288 | tf_op jit(solution)/shard_map/gather | solution.py:57
  289.0 6.0 %scatter_custom_fusion.6 = s32[2048]{0:T(1024)S(1)} fusion(s32[1024]{0:T(1024)S(1)} %get-tuple-element.652, s32[1024]{0:T(1024)S(1)} %get-tuple-element.651, s32[]{:T(128)} %constant.198.clone.1), kind=kCustom, calls=%fused_computation.107 | custom fusion | flops 1024 | bytes 8196 | tf_op jit(solution)/shard_map/scatter-max | solution.py:59
  295.1 6.2 %gather_fusion.7 = s32[1024]{0:T(1024)S(1)} fusion(s32[2048]{0:T(1024)S(1)} %scatter_custom_fusion.6, s32[1024]{0:T(1024)S(1)} %get-tuple-element.619), kind=kCustom, calls=%fused_computation.7 | custom fusion | bytes 12288 | tf_op jit(solution)/shard_map/gather | solution.py:60
  301.2 6.0 %scatter_custom_fusion.7 = s32[2048]{0:T(1024)S(1)} fusion(s32[1024]{0:T(1024)S(1)} %compare_select_fusion.11, s32[1024]{0:T(1024)S(1)} %iota_add_fusion.1, s32[]{:T(128)} %constant.203.clone.1), kind=kCustom, calls=%fused_computation.99 | custom fusion | flops 1024 | bytes 8196 | tf_op jit(solution)/shard_map/scatter-min | solution.py:64
  307.3 5.2 %all-gather.5 = s32[8192]{0:T(1024)S(1)} all-gather(s32[2048]{0:T(1024)S(1)} %scatter_custom_fusion.7), channel_id=7, replica_groups=mesh['row'=4,'col'=8] {'row'}, dimensions={0}, use_global_device_ids=true | all-gather | bytes 40960 | tf_op jit(solution)/shard_map/all_gather | solution.py:14
  312.5 5.4 %all-gather.4 = s32[8192]{0:T(1024)S(1)} all-gather(s32[2048]{0:T(1024)S(1)} %scatter_custom_fusion.6), channel_id=6, replica_groups=mesh['row'=4,'col'=8] {'row'}, dimensions={0}, use_global_device_ids=true | all-gather | bytes 40960 | tf_op jit(solution)/shard_map/all_gather | solution.py:14
  318.0 0.2 while.70
  318.2 7.1 %iota_reduce_fusion = (s32[1024]{0:T(1024)}, s32[1024]{0:T(1024)S(1)}) fusion(s32[1024,2048]{1,0:T(8,128)} %param.12, s32[2048]{0:T(1024)S(1)} %get-tuple-element.615), kind=kLoop, calls=%fused_computation.46 | loop fusion | flops 16770048 | bytes 8404992 | tf_op jit(solution)/shard_map/on_device/reduce | solution.py:43
  325.2 4.9 %select_reduce_fusion = (s32[1024]{0:T(1024)S(1)}, s32[1024]{0:T(1024)S(1)}) fusion(s32[1024,2048]{1,0:T(8,128)} %param.12, s32[1024]{0:T(1024)S(1)} %get-tuple-element.547, s32[2048]{0:T(1024)S(1)} %get-tuple-element.615), kind=kLoop, calls=%fused_computation.44 | loop fusion | flops 10483712 | bytes 8409088 | tf_op jit(solution)/shard_map/reduce_max | solution.py:44
  330.1 6.8 %pmax.124 = s32[1024]{0:T(1024)S(1)} all-reduce(s32[1024]{0:T(1024)S(1)} %get-tuple-element.551), channel_id=1, replica_groups=mesh['row'=4,'col'=8] {'col'}, use_global_device_ids=true, to_apply=%region_40.41 | all-reduce | flops 1024 | bytes 8192 | tf_op jit(solution)/shard_map/pmax | solution.py:48
  336.9 13.1 %pmin.31 = s32[1024]{0:T(1024)S(1)} all-reduce(s32[1024]{0:T(1024)S(1)} %compare_select_fusion.25), channel_id=1, replica_groups=mesh['row'=4,'col'=8] {'col'}, use_global_device_ids=true, to_apply=%region_42.43 | all-reduce | flops 1024 | bytes 8192 | tf_op jit(solution)/shard_map/pmin | solution.py:49
  350.0 6.8 %gather_fusion.8 = pred[1024]{0:T(1024)(128)(4,1)S(1)} fusion(pred[2048]{0:T(1024)(128)(4,1)S(1)} %get-tuple-element.616, s32[1024]{0:T(1024)S(1)} %get-tuple-element.617), kind=kCustom, calls=%fused_computation.8 | custom fusion | bytes 6144 | tf_op jit(solution)/shard_map/gather | solution.py:77
  356.8 11.5 %scatter_custom_fusion.8 = s32[1024]{0:T(1024)S(1)} fusion(s32[2048]{0:T(1024)S(1)} %compare_select_fusion.1, s32[2048]{0:T(1024)S(1)} %iota_add_fusion, s32[]{:T(128)} %constant.199.clone.1), kind=kCustom, calls=%fused_computation.140 | custom fusion | flops 2048 | bytes 4100 | tf_op jit(solution)/shard_map/scatter-max | solution.py:73
  368.3 33.0 %all-reduce.1 = (s32[1024]{0:T(1024)S(1)}, s32[1024]{0:T(1024)S(1)}, s32[1024]{0:T(1024)S(1)}) all-reduce(s32[1024]{0:T(1024)S(1)} %scatter_custom_fusion.8, s32[1024]{0:T(1024)S(1)} %and_convert_fusion.1, s32[1024]{0:T(1024)S(1)} %compare_select_fusion.24), channel_id=1, replica_groups=mesh['row'=4,'col'=8] {'col'}, use_global_device_ids=true, to_apply=%region_37.38 | all-reduce | flops 3072 | bytes 24576 | tf_op jit(solution)/shard_map/pmax | solution.py:78
  401.4 6.2 %gather_fusion.9 = s32[1024]{0:T(1024)S(1)} fusion(s32[2048]{0:T(1024)S(1)} %get-tuple-element.615, s32[1024]{0:T(1024)S(1)} %get-tuple-element.613), kind=kCustom, calls=%fused_computation.9 | custom fusion | bytes 12288 | tf_op jit(solution)/shard_map/gather | solution.py:57
  407.5 6.0 %scatter_custom_fusion.9 = s32[2048]{0:T(1024)S(1)} fusion(s32[1024]{0:T(1024)S(1)} %get-tuple-element.650, s32[1024]{0:T(1024)S(1)} %get-tuple-element.649, s32[]{:T(128)} %constant.198.clone.1), kind=kCustom, calls=%fused_computation.113 | custom fusion | flops 1024 | bytes 8196 | tf_op jit(solution)/shard_map/scatter-max | solution.py:59
  413.6 6.2 %gather_fusion.10 = s32[1024]{0:T(1024)S(1)} fusion(s32[2048]{0:T(1024)S(1)} %scatter_custom_fusion.9, s32[1024]{0:T(1024)S(1)} %get-tuple-element.613), kind=kCustom, calls=%fused_computation.10 | custom fusion | bytes 12288 | tf_op jit(solution)/shard_map/gather | solution.py:60
  419.8 6.0 %scatter_custom_fusion.10 = s32[2048]{0:T(1024)S(1)} fusion(s32[1024]{0:T(1024)S(1)} %compare_select_fusion.6, s32[1024]{0:T(1024)S(1)} %iota_add_fusion.1, s32[]{:T(128)} %constant.203.clone.1), kind=kCustom, calls=%fused_computation.97 | custom fusion | flops 1024 | bytes 8196 | tf_op jit(solution)/shard_map/scatter-min | solution.py:64
  425.8 5.2 %all-gather.7 = s32[8192]{0:T(1024)S(1)} all-gather(s32[2048]{0:T(1024)S(1)} %scatter_custom_fusion.10), channel_id=9, replica_groups=mesh['row'=4,'col'=8] {'row'}, dimensions={0}, use_global_device_ids=true | all-gather | bytes 40960 | tf_op jit(solution)/shard_map/all_gather | solution.py:14
  431.0 5.2 %all-gather.6 = s32[8192]{0:T(1024)S(1)} all-gather(s32[2048]{0:T(1024)S(1)} %scatter_custom_fusion.9), channel_id=8, replica_groups=mesh['row'=4,'col'=8] {'row'}, dimensions={0}, use_global_device_ids=true | all-gather | bytes 40960 | tf_op jit(solution)/shard_map/all_gather | solution.py:14
  436.2 0.2 while.71
  436.4 6.8 %gather_fusion.11 = pred[1024]{0:T(1024)(128)(4,1)S(1)} fusion(pred[2048]{0:T(1024)(128)(4,1)S(1)} %get-tuple-element.612, s32[1024]{0:T(1024)S(1)} %get-tuple-element.609), kind=kCustom, calls=%fused_computation.11 | custom fusion | bytes 6144 | tf_op jit(solution)/shard_map/gather | solution.py:77
  443.3 11.5 %scatter_custom_fusion.11 = s32[1024]{0:T(1024)S(1)} fusion(s32[2048]{0:T(1024)S(1)} %get-tuple-element.611, s32[2048]{0:T(1024)S(1)} %iota_add_fusion, s32[]{:T(128)} %constant.199.clone.1), kind=kCustom, calls=%fused_computation.138 | custom fusion | flops 2048 | bytes 4100 | tf_op jit(solution)/shard_map/scatter-max | solution.py:73
  454.8 7.0 %all-reduce = (s32[1024]{0:T(1024)S(1)}, s32[1024]{0:T(1024)S(1)}) all-reduce(s32[1024]{0:T(1024)S(1)} %scatter_custom_fusion.11, s32[1024]{0:T(1024)S(1)} %and_convert_fusion), channel_id=1, replica_groups=mesh['row'=4,'col'=8] {'col'}, use_global_device_ids=true, to_apply=%region_50.51 | all-reduce | flops 2048 | bytes 16384 | tf_op jit(solution)/shard_map/pmax | solution.py:78
  461.7 0.6 compare_select_fusion.5
  462.3 0.6 select_n.387
  (76 shorter events, 0.8 us)
Async XLA Ops:
  0.6 7.3 %copy-start = (s32[2048]{0:T(1024)S(1)}, s32[2048]{0:T(1024)}, u32[]{:S(2)}) copy-start(s32[2048]{0:T(1024)} %param.13) | copy-start | bytes 24580
  0.6 7.3 %copy-start.1 = (s32[1024,2048]{1,0:T(8,128)S(1)}, s32[1024,2048]{1,0:T(8,128)}, u32[]{:S(2)}) copy-start(s32[1024,2048]{1,0:T(8,128)} %param.12) | copy-start | bytes 25165828
  0.7 31.0 %copy-start.2 = (s32[1024]{0:T(1024)S(1)}, s32[1024]{0:T(1024)}, u32[]{:S(2)}) copy-start(s32[1024]{0:T(1024)} %param.14) | copy-start | bytes 12292
where the time goes:
time: 470 us; the launch traced here: 463 us
  blocking collectives  242 us (51%)
  other arithmetic  142 us (30%)
  local copies, waits for them, and re-layouts  76.8 us (16%)
    pmax x4, blocking collectives, on_device(): won_all, lost_all = lax.pmax((won_object, lost_here), 'col')  107 us
    another operation x4, other arithmetic, on_device(): won_object = jnp.full((pers_rows,), -1, jnp.int32).at[jnp.where(valid, wi...  46 us
    pmin x4, blocking collectives, on_device(): lax.pmin(jnp.where(local_best == best, local_target, LARGEST), 'col')  45.8 us
    all_gather x8, blocking collectives, merged(): gathered = jax.tree.map(lambda a: lax.all_gather(a, axis), part)  42.1 us
    pmax x4, blocking collectives, on_device(): best = lax.pmax(local_best, 'col')  34.7 us
    another operation x4, other arithmetic, on_device(): local_arg = jnp.argmax(value, axis=1)  28.5 us
    gather x4, local copies, waits for them, and re-layouts, on_device(): taken[jnp.clip(held_slot, 0, obj_cols - 1)]  27.2 us
    gather x4, local copies, waits for them, and re-layouts, on_device(): target_price = jnp.where(mine, price[safe_slot], 0)  24.6 us

commit v1 on v0

v1 whole, which is shorter than its diff:
```python
import functools

import jax
import jax.numpy as jnp
from jax import lax
from jax.experimental import pallas as pl
from jax.experimental.pallas import tpu as pltpu
from jax.sharding import PartitionSpec as P

ROUNDS = 4
LOWEST = -2147483647
LARGEST = 2147483647
LANES = 128
MESH = pl.DeviceIdType.MESH


def top_level_sizes(pers, objs):
    return pers // LANES, objs // LANES


def kernel(
    nrow, ncol, pers, objs,
    ben_hbm, price_in, own_in, eps_ref,
    price_out, own_out,
    ben, price, owner, one, two, lane_one, buf1, buf2, buf3, tg,
    ben_sem, s1, r1, s2, r2, s3, r3,
):
    pb_n, jb_n = top_level_sizes(pers, objs)
    row, col = lax.axis_index("row"), lax.axis_index("col")
    share = ncol // pb_n
    my_block = col // share

    loads = [
        pltpu.make_async_copy(
            ben_hbm.at[pl.ds(b * LANES, LANES)], ben.at[pl.ds(b * LANES, LANES)], ben_sem.at[b]
        )
        for b in range(pb_n)
    ]
    for load in loads:
        load.start()

    barrier = pltpu.get_barrier_semaphore()
    for k in range(1, ncol):
        pl.semaphore_signal(barrier, inc=1, device_id={"col": lax.rem(col + k, ncol)}, device_id_type=MESH)
    for k in range(1, nrow):
        pl.semaphore_signal(barrier, inc=1, device_id={"row": lax.rem(row + k, nrow)}, device_id_type=MESH)
    price[...] = price_in[...]
    owner[...] = own_in[...]
    pl.semaphore_wait(barrier, ncol - 1 + nrow - 1)

    def copy1(r, k, slot):
        return pltpu.make_async_remote_copy(
            src_ref=buf1.at[r, slot], dst_ref=buf1.at[r, slot],
            send_sem=s1.at[r, k], recv_sem=r1.at[r, slot],
            device_id={"col": lax.rem(col + k, ncol)}, device_id_type=MESH)

    def copy2(r, k, slot):
        return pltpu.make_async_remote_copy(
            src_ref=buf2.at[r, slot], dst_ref=buf2.at[r, slot],
            send_sem=s2.at[r, k], recv_sem=r2.at[r, slot],
            device_id={"row": lax.rem(row + k, nrow)}, device_id_type=MESH)

    def copy3(r, k, slot):
        return pltpu.make_async_remote_copy(
            src_ref=buf3.at[r, slot], dst_ref=buf3.at[r, slot],
            send_sem=s3.at[r, k], recv_sem=r3.at[r, slot],
            device_id={"col": lax.rem(col + k, ncol)}, device_id_type=MESH)

    sub = lax.broadcasted_iota(jnp.int32, (LANES, LANES), 0)
    lane = lax.broadcasted_iota(jnp.int32, (LANES, LANES), 1)
    group = 32

    def top_two(r):
        def block(b, _):
            @pl.when(r == 0)
            def _():
                pltpu.make_async_copy(
                    ben_hbm.at[pl.ds(b * LANES, LANES)], ben.at[pl.ds(b * LANES, LANES)], ben_sem.at[b]
                ).wait()

            for g in range(LANES // group):
                rows = pl.ds(pl.multiple_of(b * LANES + g * group, group), group)
                m1 = ben[rows, :LANES] - price[0:1, :]
                m2 = jnp.full((group, LANES), LOWEST, jnp.int32)
                at = jnp.zeros((group, LANES), jnp.int32)
                for j in range(1, jb_n):
                    v = ben[rows, j * LANES:(j + 1) * LANES] - price[j:j + 1, :]
                    more = v > m1
                    m2 = jnp.maximum(m2, jnp.where(more, m1, v))
                    at = jnp.where(more, j, at)
                    m1 = jnp.where(more, v, m1)
                here = pl.ds(g * group, group)
                one[here, :] = m1
                two[here, :] = m2
                lane_one[here, :] = at
            t1 = one[...].T
            t2 = two[...].T
            where_at = lane_one[...].T * LANES + sub
            best = jnp.max(t1, axis=0, keepdims=True)
            arg = jnp.min(jnp.where(t1 == best, where_at, LARGEST), axis=0, keepdims=True)
            second = jnp.max(jnp.where(where_at == arg, t2, t1), axis=0, keepdims=True)
            buf1[r, col, 0, pl.ds(b, 1), :] = best
            buf1[r, col, 1, pl.ds(b, 1), :] = arg
            buf1[r, col, 2, pl.ds(b, 1), :] = second
            return 0

        lax.fori_loop(0, pb_n, block, 0)

    def round_body(r, _):
        top_two(r)
        for k in range(1, ncol):
            copy1(r, k, col).start()
        for k in range(1, ncol):
            copy1(r, k, lax.rem(col + k, ncol)).wait_recv()

        best = buf1[r, 0, 0]
        for s in range(1, ncol):
            best = jnp.maximum(best, buf1[r, s, 0])
        target = jnp.full((pb_n, LANES), LARGEST, jnp.int32)
        for s in range(ncol):
            target = jnp.minimum(target, jnp.where(buf1[r, s, 0] == best, buf1[r, s, 1] + s * objs, LARGEST))
        second = jnp.full((pb_n, LANES), LOWEST, jnp.int32)
        for s in range(ncol):
            second = jnp.maximum(
                second, jnp.where(buf1[r, s, 1] + s * objs == target, buf1[r, s, 2], buf1[r, s, 0]))
        gap = best - second

        @pl.when(r > 0)
        def _():
            for k in range(1, ncol):
                copy3(r - 1, k, lax.rem(col + k, ncol)).wait_recv()
            for b in range(pb_n):
                owner[b:b + 1, :] = buf3[r - 1, b * share, 0:1, :]

        free = owner[...] < 0
        bids_on = jnp.where(free, target, -1)
        tg[0] = jnp.where(free, target, owner[...])
        tg[1] = jnp.where(free, gap, -1)
        tg[2] = jnp.where(free, target - col * objs, -1)
        buf2[r, row, jb_n:jb_n + pb_n, :] = bids_on
        buf2[r, row, jb_n + pb_n:, :] = gap

        def objects(j, _):
            acc = jnp.full((LANES, LANES), -1, jnp.int32)
            ids = sub + j * LANES
            for b in range(pb_n):
                hit = tg[2, b:b + 1, :] == ids
                acc = jnp.maximum(acc, jnp.where(hit, tg[1, b:b + 1, :], -1))
            buf2[r, row, pl.ds(j, 1), :] = jnp.max(acc.T, axis=0, keepdims=True)
            return 0

        lax.fori_loop(0, jb_n, objects, 0)
        for k in range(1, nrow):
            copy2(r, k, row).start()
        for k in range(1, nrow):
            copy2(r, k, lax.rem(row + k, nrow)).wait_recv()

        top = buf2[r, 0, :jb_n, :]
        for s in range(1, nrow):
            top = jnp.maximum(top, buf2[r, s, :jb_n, :])
        price[...] = jnp.where(top >= 0, price[...] + top + eps_ref[0], price[...])

        want = jnp.broadcast_to(tg[0, pl.ds(my_block, 1), :], (LANES, LANES)).T
        mine = jnp.broadcast_to(tg[1, pl.ds(my_block, 1), :], (LANES, LANES)).T
        me = row * pers + my_block * LANES + sub
        one[...] = jnp.zeros((LANES, LANES), jnp.int32)

        def rivals(s, _):
            beaten = one[...]
            for b in range(pb_n):
                other = s * pers + b * LANES + lane
                wish = buf2[r, s, jb_n + b:jb_n + b + 1, :]
                gaps = buf2[r, s, jb_n + pb_n + b:jb_n + pb_n + b + 1, :]
                bar = jnp.where(other < me, mine - 1, mine)
                beaten = jnp.where((wish == want) & (gaps > bar), 1, beaten)
            one[...] = beaten
            return 0

        lax.fori_loop(0, nrow, rivals, 0)
        lost = jnp.max(one[...].T, axis=0, keepdims=True)
        buf3[r, col, 0:1, :] = jnp.where(lost > 0, -1, tg[0, pl.ds(my_block, 1), :])
        for k in range(1, ncol):
            copy3(r, k, col).start()
        return 0

    lax.fori_loop(0, ROUNDS, round_body, 0)

    price_out[...] = price[...]
    for k in range(1, ncol):
        copy3(ROUNDS - 1, k, lax.rem(col + k, ncol)).wait_recv()
    for b in range(pb_n):
        own_out[b:b + 1, :] = buf3[ROUNDS - 1, b * share, 0:1, :]

    def drain(r, _):
        for k in range(1, ncol):
            copy1(r, k, col).wait_send()
            copy3(r, k, col).wait_send()
        for k in range(1, nrow):
            copy2(r, k, row).wait_send()
        return 0

    lax.fori_loop(0, ROUNDS, drain, 0)


def solution(mesh):
    nrow, ncol = mesh.shape["row"], mesh.shape["col"]

    def on_device(benefit, prices, assignment, epsilon):
        pers, objs = benefit.shape
        pb_n, jb_n = top_level_sizes(pers, objs)
        assert ncol % pb_n == 0
        vmem = pl.BlockSpec(memory_space=pltpu.VMEM)
        dma = pltpu.SemaphoreType.DMA
        price, owner = pl.pallas_call(
            functools.partial(kernel, nrow, ncol, pers, objs),
            out_shape=(
                jax.ShapeDtypeStruct((jb_n, LANES), jnp.int32),
                jax.ShapeDtypeStruct((pb_n, LANES), jnp.int32),
            ),
            in_specs=[
                pl.BlockSpec(memory_space=pl.ANY), vmem, vmem,
                pl.BlockSpec(memory_space=pltpu.SMEM),
            ],
            out_specs=(vmem, vmem),
            scratch_shapes=[
                pltpu.VMEM((pers, objs), jnp.int32),
                pltpu.VMEM((jb_n, LANES), jnp.int32),
                pltpu.VMEM((pb_n, LANES), jnp.int32),
                pltpu.VMEM((LANES, LANES), jnp.int32),
                pltpu.VMEM((LANES, LANES), jnp.int32),
                pltpu.VMEM((LANES, LANES), jnp.int32),
                pltpu.VMEM((ROUNDS, ncol, 3, pb_n, LANES), jnp.int32),
                pltpu.VMEM((ROUNDS, nrow, jb_n + 2 * pb_n, LANES), jnp.int32),
                pltpu.VMEM((ROUNDS, ncol, 8, LANES), jnp.int32),
                pltpu.VMEM((3, pb_n, LANES), jnp.int32),
                dma((pb_n,)),
                dma((ROUNDS, ncol)), dma((ROUNDS, ncol)),
                dma((ROUNDS, nrow)), dma((ROUNDS, nrow)),
                dma((ROUNDS, ncol)), dma((ROUNDS, ncol)),
            ],
            compiler_params=pltpu.CompilerParams(collective_id=0, has_side_effects=True),
            name="auction",
        )(benefit, prices.reshape(jb_n, LANES), assignment.reshape(pb_n, LANES), epsilon)
        return price.reshape(objs), owner.reshape(pers)

    return jax.shard_map(
        on_device,
        mesh=mesh,
        in_specs=(P("row", "col"), P("col"), P("row"), P()),
        out_specs=(P("col"), P("row")),
        check_vma=False,
    )
```

time: 470 us -> 71.2 us (0.15); the launches traced: 463 us -> 70.9 us
  blocking collectives: 242 us -> 0 us
  other arithmetic: 142 us -> 0 us
  local copies, waits for them, and re-layouts: 76.8 us -> 2.56 us
  Pallas kernels: 0 us -> 67 us
    pmax x9 -> x0, blocking collectives: 154 us -> none  [the longest x4 107 us: on_device(): won_all, lost_all = lax.pmax((won_object, lost_here), 'col')]
    another operation x16 -> x0, other arithmetic: 123 us -> none  [the longest x4 46 us: on_device(): won_object = jnp.full((pers_rows,), -1, jnp.int32).at[jnp.where(valid, wi...]
    gather x12 -> x0, local copies, waits for them, and re-layouts: 76.4 us -> none  [the longest x4 27.2 us: on_device(): taken[jnp.clip(held_slot, 0, obj_cols - 1)]]
    pallas_call x0 -> x1, Pallas kernels: none -> 67 us  [on_device(): pl.pallas_call(functools.partial(kernel, nrow, ncol, pers, objs), out_sha...]
    pmin x4 -> x0, blocking collectives: 45.8 us -> none  [on_device(): lax.pmin(jnp.where(local_best == best, local_target, LARGEST), 'col')]
    all_gather x8 -> x0, blocking collectives: 42.1 us -> none  [merged(): gathered = jax.tree.map(lambda a: lax.all_gather(a, axis), part)]
    reduce_max x4 -> x0, other arithmetic: 17.4 us -> none  [on_device(): jnp.max(jnp.where(columns[None, :] == local_arg[:, None], LOWEST, value),...]
where the time goes in v1:
time: 71.2 us; the launch traced here: 70.9 us
  Pallas kernels  67 us (94%)
  local copies, waits for them, and re-layouts  2.56 us (4%)
  between operations  1.29 us (2%)
    pallas_call x1, Pallas kernels, on_device(): pl.pallas_call(functools.partial(kernel, nrow, ncol, pers, objs), out_sha...  67 us
    unnamed x2, local copies, waits for them, and re-layouts  2.56 us

profile of v1, /device:TPU:0, one launch (start us, length us, event | category | flops | bytes accessed | tf_op | source)
XLA Modules:
  0.0 70.9 jit_solution(9814191350748777976)
XLA Ops:
  1.3 67.0 %auction.1 = (s32[16,128]{1,0:T(8,128)}, s32[8,128]{1,0:T(8,128)}) custom-call(s32[1024,2048]{1,0:T(8,128)} %ben_hbm.1, s32[16,128]{1,0:T(8,128)} %bitcast.4, s32[8,128]{1,0:T(8,128)} %bitcast.6, s32[1]{0:T(128)S(6)} %copy.8.eps_ref), custom_call_target="tpu_custom_call" | custom-call | tf_op jit(solution)/shard_map/auction/pallas_call | solution.py:214
  68.3 1.3 %copy.9 = s32[2048]{0:T(1024)} copy(s32[2048]{0:T(1024)} %bitcast.5) | data formatting | bytes 16384
  69.6 1.3 %copy.10 = s32[1024]{0:T(1024)} copy(s32[1024]{0:T(1024)} %bitcast.7) | data formatting | bytes 8192

commit v2 on v1

v2 whole, which is shorter than its diff:
```python
import functools

import jax
import jax.numpy as jnp
from jax import lax
from jax.experimental import pallas as pl
from jax.experimental.pallas import tpu as pltpu
from jax.sharding import PartitionSpec as P

ROUNDS = 4
LOWEST = -2147483647
LARGEST = 2147483647
LANES = 128
MESH = pl.DeviceIdType.MESH


def top_level_sizes(pers, objs):
    return pers // LANES, objs // LANES


def merge(left, right):
    b0, s0, a0 = left
    b1, s1, a1 = right
    keep = b0 >= b1
    lower = jnp.where(keep, b1, b0)
    rest = lower if s0 is None else jnp.maximum(lower, jnp.where(keep, s0, s1))
    return jnp.where(keep, b0, b1), rest, jnp.where(keep, a0, a1)


SORT8 = (
    (0, 1), (2, 3), (4, 5), (6, 7), (0, 2), (1, 3), (4, 6), (5, 7), (1, 2), (5, 6),
    (0, 4), (1, 5), (2, 6), (3, 7), (2, 4), (3, 5), (1, 2), (3, 4), (5, 6),
)


def exchanges(count):
    if count == 8:
        return SORT8
    return tuple((i, i + 1) for end in range(count - 1, 0, -1) for i in range(end))


def kernel(
    nrow, ncol, pers, objs, per_part,
    ben_hbm, price_in, own_in, eps_ref,
    price_out, own_out,
    ben, price, owner, beaten, wants, buf1, buf2, buft, buf3, tg, ranked,
    ben_sem, s1, r1, s2, r2, st, rt, s3, r3,
):
    pb_n, jb_n = top_level_sizes(pers, objs)
    parts = pb_n // per_part
    part_rows = per_part * LANES
    row, col = lax.axis_index("row"), lax.axis_index("col")
    share = ncol // pb_n
    my_block = col // share
    sub = lax.broadcasted_iota(jnp.int32, (8, LANES), 0)
    lane = lax.broadcasted_iota(jnp.int32, (8, LANES), 1)
    groups = LANES // 8

    def load(p):
        rows = pl.ds(pl.multiple_of(p * part_rows, part_rows), part_rows)
        return pltpu.make_async_copy(ben_hbm.at[rows], ben.at[rows], ben_sem.at[p])

    for p in range(parts):
        load(p).start()

    barrier = pltpu.get_barrier_semaphore()
    for k in range(1, ncol):
        pl.semaphore_signal(barrier, inc=1, device_id={"col": lax.rem(col + k, ncol)}, device_id_type=MESH)
    for k in range(1, nrow):
        pl.semaphore_signal(barrier, inc=1, device_id={"row": lax.rem(row + k, nrow)}, device_id_type=MESH)
    price[...] = price_in[...]
    owner[...] = own_in[...]
    pl.semaphore_wait(barrier, ncol - 1 + nrow - 1)

    def along_col(buf, at, send, recv, k):
        ref = buf.at[at]
        return pltpu.make_async_remote_copy(
            src_ref=ref, dst_ref=ref, send_sem=send, recv_sem=recv,
            device_id={"col": lax.rem(col + k, ncol)}, device_id_type=MESH)

    def along_row(buf, at, send, recv, k):
        ref = buf.at[at]
        return pltpu.make_async_remote_copy(
            src_ref=ref, dst_ref=ref, send_sem=send, recv_sem=recv,
            device_id={"row": lax.rem(row + k, nrow)}, device_id_type=MESH)

    def copy1(r, p, k, slot):
        return along_col(buf1, (r, p, slot, pl.ds(0, 3 * per_part)), s1.at[r, p, k], r1.at[r, p, slot], k)

    def copy2(r, k, slot):
        return along_row(buf2, (r, slot), s2.at[r, k], r2.at[r, slot], k)

    def copyt(r, k, slot):
        return along_row(buft, (r, slot), st.at[r, k], rt.at[r, slot], k)

    def copy3(r, k, slot):
        return along_col(buf3, (r, slot, pl.ds(0, 1)), s3.at[r, k], r3.at[r, slot], k)

    def row_of(ref, *at):
        return jnp.broadcast_to(ref[at], (8, LANES))

    def fold(terms, combine):
        while len(terms) > 1:
            terms = [combine(*terms[i:i + 2]) if i + 1 < len(terms) else terms[i] for i in range(0, len(terms), 2)]
        return terms[0]

    def cut(square):
        return [square[8 * g:8 * g + 8] for g in range(groups)]

    def block_top(start):
        tops = []
        for g in range(groups):
            rows = pl.ds(pl.multiple_of(start + 8 * g, 8), 8)

            def tree(lo, n):
                if n == 1:
                    return ben[rows, lo * LANES:(lo + 1) * LANES] - price[lo:lo + 1, :], None, lo
                half = n // 2
                return merge(tree(lo, half), tree(lo + half, n - half))

            m1, m2, at = tree(0, jb_n)
            tops.append((m1, m2, at * LANES + lane))
        t1, t2, ta = (cut(jnp.concatenate([t[i] for t in tops], axis=0).T) for i in range(3))

        def pick(x, y):
            (b0, s0, a0), (b1, s1_, a1) = x, y
            keep = (b0 > b1) | (b0 == b1) & (a0 < a1)
            return (
                jnp.where(keep, b0, b1),
                jnp.maximum(jnp.where(keep, b1, b0), jnp.where(keep, s0, s1_)),
                jnp.where(keep, a0, a1),
            )

        b8, s8, a8 = fold(list(zip(t1, t2, ta)), pick)
        best = jnp.max(b8, axis=0, keepdims=True)
        arg = jnp.min(jnp.where(b8 == best, a8, LARGEST), axis=0, keepdims=True)
        second = jnp.max(jnp.where(a8 == arg, s8, b8), axis=0, keepdims=True)
        return best, arg, second

    def round_body(r, _):
        def part(p, _):
            @pl.when(r == 0)
            def _():
                load(p).wait()

            for i in range(per_part):
                best, arg, second = block_top(p * part_rows + i * LANES)
                buf1[r, p, col, i:i + 1, :] = best
                buf1[r, p, col, per_part + i:per_part + i + 1, :] = arg
                buf1[r, p, col, 2 * per_part + i:2 * per_part + i + 1, :] = second
            for k in range(1, ncol):
                copy1(r, p, k, col).start()
            return 0

        lax.fori_loop(0, parts, part, 0)

        @pl.when(r > 0)
        def _():
            for k in range(1, ncol):
                copy3(r - 1, k, lax.rem(col + k, ncol)).wait_recv()
            for b in range(pb_n):
                owner[b:b + 1, :] = buf3[r - 1, b * share, 0:1, :]

        for p in range(parts):
            for k in range(1, ncol):
                copy1(r, p, k, lax.rem(col + k, ncol)).wait_recv()
            q = per_part
            bests = [buf1[r, p, s, 0:q, :] for s in range(ncol)]
            args = [buf1[r, p, s, q:2 * q, :] + s * objs for s in range(ncol)]
            best = fold(bests, jnp.maximum)
            target = fold([jnp.where(b == best, a, LARGEST) for b, a in zip(bests, args)], jnp.minimum)
            second = fold(
                [jnp.where(a == target, buf1[r, p, s, 2 * q:3 * q, :], b)
                 for s, (b, a) in enumerate(zip(bests, args))], jnp.maximum)
            here = slice(p * q, (p + 1) * q)
            held = owner[here, :]
            free = held < 0
            gap = best - second
            buft[r, row, here, :] = jnp.where(free, target, -1)
            buft[r, row, pb_n + p * q:pb_n + (p + 1) * q, :] = gap
            tg[0, here, :] = jnp.where(free, target, held)
            tg[1, here, :] = jnp.where(free, gap, -1)
        for k in range(1, nrow):
            copyt(r, k, row).start()

        pairs = []
        for b in range(pb_n):
            local = row_of(buft, r, row, slice(b, b + 1))
            pairs.append((row_of(tg, 1, slice(b, b + 1)), local - col * objs - sub))
        for i, j in exchanges(pb_n):
            (g0, d0), (g1, d1) = pairs[i], pairs[j]
            keep = g0 <= g1
            pairs[i] = (jnp.where(keep, g0, g1), jnp.where(keep, d0, d1))
            pairs[j] = (jnp.where(keep, g1, g0), jnp.where(keep, d1, d0))
        for b in range(pb_n):
            ranked[0, b], ranked[1, b] = pairs[b]

        def objects(j, _):
            gaps = [ranked[0, b] for b in range(pb_n)]
            offs = [ranked[1, b] - j * LANES for b in range(pb_n)]
            rows = []
            for g in range(groups):
                acc = jnp.full((8, LANES), -1, jnp.int32)
                for gap_b, off in zip(gaps, offs):
                    acc = jnp.where(off == 8 * g, gap_b, acc)
                rows.append(acc)
            top = fold(cut(jnp.concatenate(rows, axis=0).T), jnp.maximum)
            buf2[r, row, pl.ds(j, 1), :] = jnp.max(top, axis=0, keepdims=True)
            return 0

        lax.fori_loop(0, jb_n, objects, 0, unroll=2)
        for k in range(1, nrow):
            copy2(r, k, row).start()

        wants[0] = jnp.broadcast_to(tg[0, pl.ds(my_block, 1), :], (LANES, LANES)).T
        wants[1] = jnp.broadcast_to(tg[1, pl.ds(my_block, 1), :], (LANES, LANES)).T
        wish = row_of(buft, r, row, pl.ds(my_block, 1))
        gaps = row_of(buft, r, row, pl.ds(pb_n + my_block, 1))
        for g in range(groups):
            at = slice(8 * g, 8 * g + 8)
            tie = (wish == wants[0, at]) & (gaps == wants[1, at]) & (lane < sub + 8 * g)
            beaten[at, :] = jnp.where(tie, 1, 0)

        def rivals(i, _):
            s = lax.rem(row + i, nrow)

            @pl.when(i > 0)
            def _():
                copyt(r, nrow - i, s).wait_recv()

            wishes, lifts = [], []
            for b in range(pb_n):
                ahead = s * pers + b * LANES < row * pers + my_block * LANES
                wishes.append(row_of(buft, r, s, slice(b, b + 1)))
                lifts.append(row_of(buft, r, s, slice(pb_n + b, pb_n + b + 1)) + jnp.where(ahead, 1, 0))
            for g in range(groups):
                at = slice(8 * g, 8 * g + 8)
                want, mine, acc = wants[0, at], wants[1, at], beaten[at, :]
                for w, lift in zip(wishes, lifts):
                    acc = jnp.where((w == want) & (lift > mine), 1, acc)
                beaten[at, :] = acc
            return 0

        lax.fori_loop(0, nrow, rivals, 0)
        lost = jnp.max(fold(cut(beaten[...].T), jnp.bitwise_or), axis=0, keepdims=True)
        buf3[r, col, 0:1, :] = jnp.where(lost > 0, -1, tg[0, pl.ds(my_block, 1), :])
        for k in range(1, ncol):
            copy3(r, k, col).start()

        for k in range(1, nrow):
            copy2(r, k, lax.rem(row + k, nrow)).wait_recv()
        top = fold([buf2[r, s] for s in range(nrow)], jnp.maximum)
        price[...] = jnp.where(top >= 0, price[...] + top + eps_ref[0], price[...])
        return 0

    lax.fori_loop(0, ROUNDS, round_body, 0)

    price_out[...] = price[...]
    for k in range(1, ncol):
        copy3(ROUNDS - 1, k, lax.rem(col + k, ncol)).wait_recv()
    for b in range(pb_n):
        own_out[b:b + 1, :] = buf3[ROUNDS - 1, b * share, 0:1, :]

    def drain(r, _):
        for k in range(1, ncol):
            for p in range(parts):
                copy1(r, p, k, col).wait_send()
            copy3(r, k, col).wait_send()
        for k in range(1, nrow):
            copy2(r, k, row).wait_send()
            copyt(r, k, row).wait_send()
        return 0

    lax.fori_loop(0, ROUNDS, drain, 0)


def solution(mesh):
    nrow, ncol = mesh.shape["row"], mesh.shape["col"]

    def on_device(benefit, prices, assignment, epsilon):
        pers, objs = benefit.shape
        pb_n, jb_n = top_level_sizes(pers, objs)
        assert ncol % pb_n == 0
        per_part = 2
        parts = pb_n // per_part
        vmem = pl.BlockSpec(memory_space=pltpu.VMEM)
        dma = pltpu.SemaphoreType.DMA
        price, owner = pl.pallas_call(
            functools.partial(kernel, nrow, ncol, pers, objs, per_part),
            out_shape=(
                jax.ShapeDtypeStruct((jb_n, LANES), jnp.int32),
                jax.ShapeDtypeStruct((pb_n, LANES), jnp.int32),
            ),
            in_specs=[
                pl.BlockSpec(memory_space=pl.ANY), vmem, vmem,
                pl.BlockSpec(memory_space=pltpu.SMEM),
            ],
            out_specs=(vmem, vmem),
            scratch_shapes=[
                pltpu.VMEM((pers, objs), jnp.int32),
                pltpu.VMEM((jb_n, LANES), jnp.int32),
                pltpu.VMEM((pb_n, LANES), jnp.int32),
                pltpu.VMEM((LANES, LANES), jnp.int32),
                pltpu.VMEM((2, LANES, LANES), jnp.int32),
                pltpu.VMEM((ROUNDS, parts, ncol, 8, LANES), jnp.int32),
                pltpu.VMEM((ROUNDS, nrow, jb_n, LANES), jnp.int32),
                pltpu.VMEM((ROUNDS, nrow, 2 * pb_n, LANES), jnp.int32),
                pltpu.VMEM((ROUNDS, ncol, 8, LANES), jnp.int32),
                pltpu.VMEM((2, pb_n, LANES), jnp.int32),
                pltpu.VMEM((2, pb_n, 8, LANES), jnp.int32),
                dma((parts,)),
                dma((ROUNDS, parts, ncol)), dma((ROUNDS, parts, ncol)),
                dma((ROUNDS, nrow)), dma((ROUNDS, nrow)),
                dma((ROUNDS, nrow)), dma((ROUNDS, nrow)),
                dma((ROUNDS, ncol)), dma((ROUNDS, ncol)),
            ],
            compiler_params=pltpu.CompilerParams(collective_id=0, has_side_effects=True),
            name="auction",
        )(benefit, prices.reshape(jb_n, LANES), assignment.reshape(pb_n, LANES), epsilon)
        return price.reshape(objs), owner.reshape(pers)

    return jax.shard_map(
        on_device,
        mesh=mesh,
        in_specs=(P("row", "col"), P("col"), P("row"), P()),
        out_specs=(P("col"), P("row")),
        check_vma=False,
    )
```

time: 71.2 us -> 60.8 us (0.85)
  Pallas kernels: 67 us -> 56.6 us
    pallas_call x1, Pallas kernels: 67 us -> 56.6 us  [on_device(): pl.pallas_call(functools.partial(kernel, nrow, ncol, pers, objs, per_part...]
where the time goes in v2:
time: 60.8 us; the launch traced here: 60.4 us
  Pallas kernels  56.6 us (93%)
  local copies, waits for them, and re-layouts  2.56 us (4%)
  between operations  1.29 us (2%)
    pallas_call x1, Pallas kernels, on_device(): pl.pallas_call(functools.partial(kernel, nrow, ncol, pers, objs, per_part...  56.6 us
    unnamed x2, local copies, waits for them, and re-layouts  2.56 us

profile of v2, /device:TPU:0, one launch (start us, length us, event | category | flops | bytes accessed | tf_op | source)
XLA Modules:
  0.0 60.4 jit_solution(8783834456654833793)
XLA Ops:
  1.3 56.6 %auction.1 = (s32[16,128]{1,0:T(8,128)}, s32[8,128]{1,0:T(8,128)}) custom-call(s32[1024,2048]{1,0:T(8,128)} %ben_hbm.1, s32[16,128]{1,0:T(8,128)} %bitcast.4, s32[8,128]{1,0:T(8,128)} %bitcast.6, s32[1]{0:T(128)S(6)} %copy.8.eps_ref), custom_call_target="tpu_custom_call" | custom-call | tf_op jit(solution)/shard_map/auction/pallas_call | solution.py:288
  57.9 1.3 %copy.9 = s32[2048]{0:T(1024)} copy(s32[2048]{0:T(1024)} %bitcast.5) | data formatting | bytes 16384
  59.1 1.3 %copy.10 = s32[1024]{0:T(1024)} copy(s32[1024]{0:T(1024)} %bitcast.7) | data formatting | bytes 8192

commit v3 on v2

--- a/solution.py
+++ b/solution.py
@@ -70,7 +70,6 @@
         pl.semaphore_signal(barrier, inc=1, device_id={"row": lax.rem(row + k, nrow)}, device_id_type=MESH)
     price[...] = price_in[...]
     owner[...] = own_in[...]
-    pl.semaphore_wait(barrier, ncol - 1 + nrow - 1)
 
     def along_col(buf, at, send, recv, k):
         ref = buf.at[at]
@@ -148,6 +147,11 @@
                 buf1[r, p, col, i:i + 1, :] = best
                 buf1[r, p, col, per_part + i:per_part + i + 1, :] = arg
                 buf1[r, p, col, 2 * per_part + i:2 * per_part + i + 1, :] = second
+
+            @pl.when((r == 0) & (p == 0))
+            def _():
+                pl.semaphore_wait(barrier, ncol - 1 + nrow - 1)
+
             for k in range(1, ncol):
                 copy1(r, p, k, col).start()
             return 0
@@ -281,7 +285,7 @@
         pers, objs = benefit.shape
         pb_n, jb_n = top_level_sizes(pers, objs)
         assert ncol % pb_n == 0
-        per_part = 2
+        per_part = 4
         parts = pb_n // per_part
         vmem = pl.BlockSpec(memory_space=pltpu.VMEM)
         dma = pltpu.SemaphoreType.DMA
@@ -302,7 +306,7 @@
                 pltpu.VMEM((pb_n, LANES), jnp.int32),
                 pltpu.VMEM((LANES, LANES), jnp.int32),
                 pltpu.VMEM((2, LANES, LANES), jnp.int32),
-                pltpu.VMEM((ROUNDS, parts, ncol, 8, LANES), jnp.int32),
+                pltpu.VMEM((ROUNDS, parts, ncol, 16, LANES), jnp.int32),
                 pltpu.VMEM((ROUNDS, nrow, jb_n, LANES), jnp.int32),
                 pltpu.VMEM((ROUNDS, nrow, 2 * pb_n, LANES), jnp.int32),
                 pltpu.VMEM((ROUNDS, ncol, 8, LANES), jnp.int32),

time: 60.8 us -> 60.3 us (level)
  no operation moved by 1% of the time
where the time goes in v3:
time: 60.3 us; the launch traced here: 59.9 us
  Pallas kernels  56.1 us (93%)
  local copies, waits for them, and re-layouts  2.56 us (4%)
  between operations  1.29 us (2%)
    pallas_call x1, Pallas kernels, on_device(): pl.pallas_call(functools.partial(kernel, nrow, ncol, pers, objs, per_part...  56.1 us
    unnamed x2, local copies, waits for them, and re-layouts  2.56 us

profile of v3, /device:TPU:0, one launch (start us, length us, event | category | flops | bytes accessed | tf_op | source)
XLA Modules:
  0.0 59.9 jit_solution(6832556548408986697)
XLA Ops:
  1.3 56.1 %auction.1 = (s32[16,128]{1,0:T(8,128)}, s32[8,128]{1,0:T(8,128)}) custom-call(s32[1024,2048]{1,0:T(8,128)} %ben_hbm.1, s32[16,128]{1,0:T(8,128)} %bitcast.4, s32[8,128]{1,0:T(8,128)} %bitcast.6, s32[1]{0:T(128)S(6)} %copy.8.eps_ref), custom_call_target="tpu_custom_call" | custom-call | tf_op jit(solution)/shard_map/auction/pallas_call | solution.py:292
  57.4 1.3 %copy.9 = s32[2048]{0:T(1024)} copy(s32[2048]{0:T(1024)} %bitcast.5) | data formatting | bytes 16384
  58.7 1.3 %copy.10 = s32[1024]{0:T(1024)} copy(s32[1024]{0:T(1024)} %bitcast.7) | data formatting | bytes 8192
